TPU v7x, 128 devices: a whole 4x4x4 slice. The times are simulated.
128 devices in a mesh: tp: 16 (over z, x_hi, core), fs: 8 (over y, x_lo).
Axes of the slice: x: 4 (x_hi: 2, x_lo: 2; x = x_hi * 2 + x_lo), y: 4, z: 4, core: 2. Of those that a mesh axis runs over, the one named last changes fastest.
Arguments:
- tokens: bfloat16 [512, 8192], P(('tp', 'fs')), may hold values from -6 to 6
- gate_weight: bfloat16 [8192, 29568], P('fs', 'tp'), may hold values from -0.0625 to 0.0625
- up_weight: bfloat16 [8192, 29568], P('fs', 'tp'), may hold values from -0.0625 to 0.0625
- down_weight: bfloat16 [29568, 8192], P('tp', 'fs'), may hold values from -0.046875 to 0.046875
Outputs:
- mixed: bfloat16 [512, 8192], P(None, ('fs', 'tp'))
All inputs are finite; a program needn't handle non-finite values.
Results may differ from a plain program's by a relative error of at most 0.0049.
Values may be sent and summed in bfloat16 or wider, within the bound.
A program may use at most 64 MiB of HBM per device.

v0:
```python
import jax
import jax.numpy as jnp
from jax import lax
from jax.sharding import Mesh
from jax.sharding import PartitionSpec as P

FS = ("fs_0", "fs_1")
TP_FS = ("tp", "fs_0", "fs_1")
FS_TP = ("fs_0", "fs_1", "tp")


def laid_out(pieces, dim):
    dims = list(pieces.shape[1:])
    dims[dim] *= pieces.shape[0]
    return jnp.moveaxis(pieces, 0, dim).reshape(dims)


def copy_for_each(shard, axis):
    copies = jnp.broadcast_to(shard, (lax.axis_size(axis), *shard.shape))
    return lax.all_to_all(copies, axis, split_axis=0, concat_axis=0, tiled=True)


def gather_directly(shard, axis, dim):
    return laid_out(copy_for_each(shard, axis), dim)


def sum_by_axis(shard, axes, dim):
    for axis in axes:
        shard = lax.psum_scatter(shard, axis, scatter_dimension=dim, tiled=True)
    return shard


def cut_along(shard, dim, count):
    before, after = (shard.shape[:dim], shard.shape[dim + 1 :])
    return jnp.moveaxis(shard.reshape(*before, count, -1, *after), dim, 0)


def sent_and_summed(shard, axis, dim):
    pieces = cut_along(shard, dim, lax.axis_size(axis))
    arrived = lax.all_to_all(pieces, axis, split_axis=0, concat_axis=0, tiled=True)
    return arrived.sum(axis=0)


def body(tokens, gate_weight, up_weight, down_weight):
    by_feature = lax.all_to_all(tokens, FS, split_axis=1, concat_axis=0, tiled=True)
    feature_rows = gather_directly(by_feature, "tp", 0)
    gate_part = jnp.dot(feature_rows, gate_weight, preferred_element_type=jnp.float32)
    up_part = jnp.dot(feature_rows, up_weight, preferred_element_type=jnp.float32)
    gate, up = (sum_by_axis(gate_part, FS, 1), sum_by_axis(up_part, FS, 1))
    hidden = (jax.nn.silu(gate) * up).astype(jnp.bfloat16)
    group_hidden = gather_directly(hidden, FS, 1)
    partial_cols = jnp.dot(group_hidden, down_weight, preferred_element_type=jnp.float32)
    summed = sent_and_summed(partial_cols, "tp", 1)
    return summed.astype(jnp.bfloat16)


def solution(mesh):
    finer = Mesh(mesh.devices.reshape(mesh.shape["tp"], 4, 2), ("tp", "fs_0", "fs_1"))
    in_specs = (P(TP_FS, None), P(FS, "tp"), P(FS, "tp"), P("tp", FS))
    out_specs = P(None, FS_TP)
    return jax.shard_map(body, mesh=finer, in_specs=in_specs, out_specs=out_specs, check_vma=False)
```

profile of v0, /device:TPU:1, one launch (start us, length us, event | category | flops | bytes accessed | tf_op | source)
XLA Modules:
  0.0 244.5 jit_solution(6208779732393416822)
XLA Ops:
  0.0 11.1 %all_to_all.34 = bf16[4,8,1024]{2,0,1:T(4,128)(2,1)S(1)} all-to-all(bf16[4,8,1024]{2,0,1:T(4,128)(2,1)} %bitcast.34), channel_id=1, replica_groups=mesh['tp'=16,'fs_0'=4,'fs_1'=2] {'fs_0','fs_1'}, dimensions={1} | all-to-all | bytes 131072 | tf_op jit(solution)/shard_map/all_to_all | solution.py:45
  11.3 26.2 %all_to_all.35 = bf16[16,32,1024]{2,1,0:T(8,128)(2,1)S(1)} all-to-all(bf16[16,32,1024]{2,1,0:T(8,128)(2,1)S(1)} %broadcast_in_dim.6), channel_id=1, replica_groups=mesh['tp'=16,'fs_0'=4,'fs_1'=2] {'tp'}, dimensions={0} | all-to-all | bytes 2097152 | tf_op jit(solution)/shard_map/all_to_all | solution.py:20
  37.5 6.3 %fusion.7 = f32[512,1848]{0,1:T(8,128)} fusion(bf16[512,1024]{1,0:T(8,128)(2,1)S(1)} %bitcast.31, bf16[1024,1848]{0,1:T(8,128)(2,1)} %param.5), kind=kOutput, calls=%fused_computation.5 | convolution fusion | flops 1937768448 | bytes 8617984 | tf_op jit(solution)/shard_map/dot_general | solution.py:47
  43.7 4.1 %fusion.8 = f32[512,1848]{0,1:T(8,128)} fusion(bf16[512,1024]{1,0:T(8,128)(2,1)S(1)} %bitcast.32, bf16[1024,1848]{0,1:T(8,128)(2,1)S(1)} %copy-done.3), kind=kOutput, calls=%fused_computation.6 | convolution fusion | flops 1937768448 | bytes 8617984 | tf_op jit(solution)/shard_map/dot_general | solution.py:48
  47.8 87.6 %fusion.5 = (f32[512,464]{0,1:T(8,128)S(1)}, f32[512,464]{0,1:T(8,128)S(1)}) fusion(f32[512,1848]{0,1:T(8,128)} %fusion.8, f32[512,1848]{0,1:T(8,128)} %fusion.7), kind=kCustom, calls=%all-reduce-scatter.4 | all-reduce-scatter fusion | flops 1900545 | bytes 9470464
  135.4 1.6 collective-permute-start
  137.0 0.6 dynamic-slice.10
  138.3 2.5 %collective-permute-start.2 = (f32[512,6]{0,1:T(8,128)S(1)}, f32[512,6]{0,1:T(8,128)S(1)}, u32[]{:S(2)}, u32[]{:S(2)}) collective-permute-start(f32[512,6]{0,1:T(8,128)S(1)} %slice.2), channel_id=1, source_target_pairs={{0,2},{2,4},{4,6},{1,3},{3,5},{5,7},{8,10},{10,12},{12,14},{9,11},... | collective-permute-start | bytes 36872
  140.8 1.3 concatenate
  142.1 1.1 constant_dynamic-slice_fusion.1
  143.2 1.3 concatenate.2
  144.7 22.0 %fusion.6 = (f32[512,232]{0,1:T(8,128)S(1)}, f32[512,232]{0,1:T(8,128)S(1)}) fusion(f32[512,462]{0,1:T(8,128)S(1)} %constant_dynamic-slice_fusion, f32[512,462]{0,1:T(8,128)S(1)} %copy-done), kind=kCustom, calls=%all-reduce-scatter.5 | all-reduce-scatter fusion | flops 475137 | bytes 2843136
  166.8 2.1 collective-permute-start.1
  168.9 1.3 collective-permute-start.3
  170.2 0.6 dynamic-slice.14
  171.5 0.4 concatenate.1
  172.4 1.4 broadcast_in_dim.7
  173.8 3.6 %all-to-all-start.2 = ((bf16[8,512,231]{1,2,0:T(8,128)(2,1)}), bf16[8,512,231]{1,2,0:T(8,128)(2,1)S(1)}, u32[]{:S(2)}, u32[]{:S(2)}) async-start(bf16[8,512,231]{1,2,0:T(8,128)(2,1)} %broadcast_in_dim.7), calls=%async_computation.2 | async-start | bytes 3801088 | tf_op jit(solution)/shard_map/all_to_all | solution.py:20
  177.4 6.0 %copy.9 = bf16[1848,1024]{0,1:T(8,128)(2,1)} copy(bf16[1848,1024]{1,0:T(8,128)(2,1)} %param.7) | data formatting | bytes 7569408 | tf_op args[3]
  183.4 15.2 %all-to-all-done.2 = bf16[8,512,231]{1,2,0:T(8,128)(2,1)S(1)} async-done(((bf16[8,512,231]{1,2,0:T(8,128)(2,1)}), bf16[8,512,231]{1,2,0:T(8,128)(2,1)S(1)}, u32[]{:S(2)}, u32[]{:S(2)}) %all-to-all-start.2) | async-done | bytes 1892384 | tf_op jit(solution)/shard_map/all_to_all | solution.py:20
  198.6 1.8 reshape.13
  200.5 5.0 %convolution_bitcast_fusion = f32[16,512,64]{1,2,0:T(8,128)S(1)} fusion(bf16[512,1848,1]{0,1,2:T(8,128)(2,1)} %reshape.13, bf16[16,64,1848]{2,1,0:T(8,128)(2,1)} %bitcast.30), kind=kOutput, calls=%fused_computation | convolution fusion | flops 1937768448 | bytes 7774208 | tf_op jit(solution)/shard_map/dot_general | solution.py:52
  205.5 38.2 %all_to_all.36 = f32[16,512,64]{1,2,0:T(8,128)S(1)} all-to-all(f32[16,512,64]{1,2,0:T(8,128)S(1)} %convolution_bitcast_fusion), channel_id=1, replica_groups=mesh['tp'=16,'fs_0'=4,'fs_1'=2] {'tp'}, dimensions={0} | all-to-all | bytes 4194304 | tf_op jit(solution)/shard_map/all_to_all | solution.py:40
  243.7 0.8 reduce_sum.9
  (21 shorter events, 0.8 us)
Async XLA Ops:
  37.4 6.3 %copy-start.3 = (bf16[1024,1848]{0,1:T(8,128)(2,1)S(1)}, bf16[1024,1848]{0,1:T(8,128)(2,1)}, u32[]{:S(2)}) copy-start(bf16[1024,1848]{0,1:T(8,128)(2,1)} %param.6) | copy-start | bytes 11354116
  47.8 89.2 %copy-start.2 = (u32[128]{0:T(128)S(1)}, u32[128]{0:T(128)}, u32[]{:S(2)}) copy-start(u32[128]{0:T(128)} %constant.11) | copy-start | bytes 1540
  135.4 5.3 %collective-permute-start = (f32[512,6]{0,1:T(8,128)S(1)}, f32[512,6]{0,1:T(8,128)S(1)}, u32[]{:S(2)}, u32[]{:S(2)}) collective-permute-start(f32[512,6]{0,1:T(8,128)S(1)} %slice), channel_id=1, source_target_pairs={{0,2},{2,4},{4,6},{1,3},{3,5},{5,7},{8,10},{10,12},{12,14},{9,11},... | collective-permute-start | bytes 36872
  138.3 4.9 %collective-permute-start.2 = (f32[512,6]{0,1:T(8,128)S(1)}, f32[512,6]{0,1:T(8,128)S(1)}, u32[]{:S(2)}, u32[]{:S(2)}) collective-permute-start(f32[512,6]{0,1:T(8,128)S(1)} %slice.2), channel_id=1, source_target_pairs={{0,2},{2,4},{4,6},{1,3},{3,5},{5,7},{8,10},{10,12},{12,14},{9,11},... | collective-permute-start | bytes 36872
  143.2 1.5 copy-start
  143.2 27.0 %copy-start.1 = (u32[128]{0:T(128)S(1)}, u32[128]{0:T(128)}, u32[]{:S(2)}) copy-start(u32[128]{0:T(128)} %constant.15) | copy-start | bytes 1540
  166.8 4.7 %collective-permute-start.1 = (f32[512,1]{0,1:T(1,128)S(1)}, f32[512,1]{0,1:T(1,128)S(1)}, u32[]{:S(2)}, u32[]{:S(2)}) collective-permute-start(f32[512,1]{0,1:T(1,128)S(1)} %slice.1), channel_id=1, source_target_pairs={{0,1},{2,3},{4,5},{6,7},{8,9},{10,11},{12,13},{14,15},{16,17},{18,... | collective-permute-start | bytes 6152
  168.9 2.9 %collective-permute-start.3 = (f32[512,1]{0,1:T(1,128)S(1)}, f32[512,1]{0,1:T(1,128)S(1)}, u32[]{:S(2)}, u32[]{:S(2)}) collective-permute-start(f32[512,1]{0,1:T(1,128)S(1)} %slice.3), channel_id=1, source_target_pairs={{0,1},{2,3},{4,5},{6,7},{8,9},{10,11},{12,13},{14,15},{16,17},{18,... | collective-permute-start | bytes 6152
  173.8 24.9 %all-to-all-start.2 = ((bf16[8,512,231]{1,2,0:T(8,128)(2,1)}), bf16[8,512,231]{1,2,0:T(8,128)(2,1)S(1)}, u32[]{:S(2)}, u32[]{:S(2)}) async-start(bf16[8,512,231]{1,2,0:T(8,128)(2,1)} %broadcast_in_dim.7), calls=%async_computation.2 | async-start | bytes 3801088 | tf_op jit(solution)/shard_map/all_to_all | solution.py:20
where the time goes:
time: 245 us; the launch traced here: 244 us
  blocking collectives  185 us (76%)
  matrix products  15.4 us (6%)
  local copies, waits for them, and re-layouts  15.2 us (6%)
  waiting for transfers between devices  15.2 us (6%)
  starting transfers between devices  11 us (4%)
    unnamed x2, blocking collectives  110 us
    all_to_all x1, blocking collectives, sent_and_summed(): lax.all_to_all(pieces, axis, split_axis=0, concat_axis=0, tiled=True)  38.2 us
    all_to_all x1, blocking collectives, copy_for_each(): return lax.all_to_all(copies, axis, split_axis=0, concat_axis=0, tiled=True)  26.2 us
    all_to_all x1, waiting for transfers between devices, copy_for_each(): return lax.all_to_all(copies, axis, split_axis=0, concat_axis=0, tiled=True)  15.2 us
    unnamed x21, local copies, waits for them, and re-layouts  11.8 us
    all_to_all x1, blocking collectives, body(): lax.all_to_all(tokens, FS, split_axis=1, concat_axis=0, tiled=True)  11.1 us
    unnamed x4, starting transfers between devices  7.45 us
    dot_general x1, matrix products, body(): jnp.dot(feature_rows, gate_weight, preferred_element_type=jnp.float32)  6.28 us
  transfers between devices with their start and end apart: 5, of which 1 were waited for; matrix products, arithmetic and copies ran while one was open for 4% of the time, Pallas kernels for 0%

commit v1 on v0

v1 whole, which is shorter than its diff:
```python
import functools

import jax
import jax.numpy as jnp
from jax import lax
from jax.experimental import pallas as pl
from jax.experimental.pallas import tpu as pltpu
from jax.sharding import PartitionSpec as P

BF = jnp.bfloat16
F32 = jnp.float32
MESH = pl.DeviceIdType.MESH

FAR, EARLY, LATE, XS, HY, HF, HX, DD = 0, 2, 4, 6, 7, 9, 11, 15
SPLIT = 1024
PLAN = (
    "M0 A0 B0 M1",
    "A1 C0 B1 D0",
    "M2 A2 E0 C1",
    "B2 F0 D1 M3",
    "A3 E1 G0 C2",
    "B3 I0 F1 D2",
    "G1 E2 C3 I1",
    "F2 D3 G2 E3",
    "I2 F3 G3 I3",
)


def kernel(tok, wg_hbm, wu_hbm, wd_hbm, out, wg, wu, wd, slab, x, pf, sf, far_s, far_r, early_s, early_r,
           late_s, late_r, xs_s, xs_r, keep, hb, mf, dd_s, dd_r, mb, mr, own, fin_s, fin_r,
           wsem, t1s, t1r, t2s, t2r, zs, zr, rs, rr, ms, mrs, fs_sem, fr_sem):
    f = lax.axis_index("fs")
    t = lax.axis_index("tp")
    y, xl = f // 2, f % 2
    z, xh, core = t // 4, (t // 2) % 2, t % 2
    chip = t // 2
    ff = pf.shape[-1]

    def fs_dev(yy, xx):
        return {"fs": (yy % 4) * 2 + xx, "tp": t}

    def tp_dev(zz, hh, cc):
        return {"fs": f, "tp": (zz % 4) * 4 + hh * 2 + cc}

    loads = [pltpu.make_async_copy(a, b, wsem.at[i]) for i, (a, b) in enumerate(((wg_hbm, wg), (wu_hbm, wu), (wd_hbm, wd)))]
    for c in loads:
        c.start()

    ydev = (fs_dev(y + 1, xl), fs_dev(y + 3, xl))
    xdev = fs_dev(y, 1 - xl)
    cdev = tp_dev(z, xh, 1 - core)
    zdev = (tp_dev(z + 1, xh, core), tp_dev(z + 3, xh, core))
    fs_all = [{"fs": (f + k) % 8, "tp": t} for k in range(1, 8)]
    chips = [{"fs": f, "tp": ((chip + k) % 8) * 2 + core} for k in range(1, 8)]
    block = [cdev, tp_dev(z, 1 - xh, core), tp_dev(z, 1 - xh, 1 - core)]

    barrier = pltpu.get_barrier_semaphore()
    peers = fs_all + chips + [block[0], block[2]]
    for d in peers:
        pl.semaphore_signal(barrier, inc=1, device_id=d, device_id_type=MESH)
    pl.semaphore_wait(barrier, len(peers))

    sent = []

    def send(src, dst, ssem, rsem, dev):
        c = pltpu.make_async_remote_copy(src_ref=src, dst_ref=dst, send_sem=ssem, recv_sem=rsem, device_id=dev, device_id_type=MESH)
        c.start()
        sent.append(c)
        return c

    t1 = []
    for k in range(1, 8):
        g = (f + k) % 8
        cols = pl.ds(pl.multiple_of(g * 1024, 1024), 1024)
        t1.append(send(tok.at[:, cols], slab.at[f], t1s.at[k - 1], t1r.at[k - 1], fs_all[k - 1]))
    slab[f] = tok[:, pl.ds(pl.multiple_of(f * 1024, 1024), 1024)]
    for c in t1:
        c.wait_recv()
    quarter = xh * 2 + core
    rows32 = pl.ds(pl.multiple_of(quarter * 32, 32), 32)
    x[z, rows32, :] = slab[...].astype(F32).reshape(32, 1024).astype(BF)
    t2 = [send(x.at[z, rows32], x.at[z, rows32], t2s.at[k], t2r.at[k], block[k]) for k in range(3)]

    zb = (z, (z + 3) % 4, (z + 1) % 4, (z + 2) % 4)
    r32 = lambda yy: pl.ds(pl.multiple_of((yy % 4) * 32, 32), 32)
    r16 = lambda yy, xx: pl.ds(pl.multiple_of((yy % 4) * 32 + xx * 16, 16), 16)
    zc = {}

    def M(i):
        if i == 0:
            for c in t2:
                c.wait_recv()
            zc[0] = send(x.at[z], x.at[z], zs.at[0], zr.at[0], zdev[0])
            zc[1] = send(x.at[z], x.at[z], zs.at[1], zr.at[1], zdev[1])
            loads[0].wait()
            loads[1].wait()
        elif i == 1:
            zc[0].wait_recv()
            half = x.at[zb[1], pl.ds(0, 64)]
            zc[2] = send(half, half, zs.at[2], zr.at[2], zdev[0])
        elif i == 2:
            zc[1].wait_recv()
            half = x.at[zb[2], pl.ds(64, 64)]
            zc[3] = send(half, half, zs.at[3], zr.at[3], zdev[1])
        else:
            zc[2].wait_recv()
            zc[3].wait_recv()
        xi = x[zb[i]]
        pf[i, 0] = jnp.dot(xi, wg[...], preferred_element_type=F32)
        pf[i, 1] = jnp.dot(xi, wu[...], preferred_element_type=F32)

    rc = {}

    def rsend(i, k, src, dst, dev):
        rc[i, k] = send(src, dst, rs.at[i, k], rr.at[i, k], dev)

    def A(i):
        for d in (0, 1):
            far_s[i, d] = pf[i, :, r16(y + 2, d), :].astype(BF)
            rsend(i, FAR + d, far_s.at[i, d], far_r.at[i, d], ydev[d])
        for d in (0, 1):
            early_s[i, d] = pf[i, :, r16(y + 1 + 2 * d, 1 - d), :].astype(BF)
            rsend(i, EARLY + d, early_s.at[i, d], early_r.at[i, d], ydev[d])

    def B(i):
        for d in (0, 1):
            rc[i, FAR + d].wait_recv()
            late_s[i, d] = (pf[i, :, r16(y + 1 + 2 * d, d), :] + far_r[i, d].astype(F32)).astype(BF)
            rsend(i, LATE + d, late_s.at[i, d], late_r.at[i, d], ydev[d])

    def C(i):
        for k in (EARLY, EARLY + 1, LATE, LATE + 1):
            rc[i, k].wait_recv()
        sf[0] = pf[i, :, r16(y, 0), :] + late_r[i, 0].astype(F32) + early_r[i, 1].astype(F32)
        sf[1] = pf[i, :, r16(y, 1), :] + early_r[i, 0].astype(F32) + late_r[i, 1].astype(F32)
        xs_s[i] = sf[1 - xl].astype(BF)
        rsend(i, XS, xs_s.at[i], xs_r.at[i], xdev)
        keep[i] = sf[xl]

    def hrow(i, yy, xx):
        return hb.at[i, r16(yy, xx)]

    def D(i):
        rc[i, XS].wait_recv()
        gu = keep[i] + xs_r[i].astype(F32)
        g, u = gu[0], gu[1]
        hb[i, r16(y, xl), :] = (g / (1.0 + jnp.exp(-g)) * u).astype(BF)
        piece = hrow(i, y, xl)
        rsend(i, HY, piece, piece, ydev[0])
        rsend(i, HY + 1, piece, piece, ydev[1])
        rsend(i, HX, piece, piece, xdev)

    def E(i):
        for d in (0, 1):
            rc[i, HY + d].wait_recv()
            yy = y + 3 - 2 * d
            cols = pl.ds(0, SPLIT) if d == 0 else pl.ds(SPLIT, ff - SPLIT)
            part = hb.at[i, r16(yy, xl), cols]
            rsend(i, HF + d, part, part, ydev[d])
            piece = hrow(i, yy, xl)
            rsend(i, HX + 1 + d, piece, piece, xdev)

    def F(i):
        rc[i, HF].wait_recv()
        rc[i, HF + 1].wait_recv()
        piece = hrow(i, y + 2, xl)
        rsend(i, HX + 3, piece, piece, xdev)

    def G(i):
        if i == 0:
            loads[2].wait()
        for k in range(4):
            rc[i, HX + k].wait_recv()
        mf[i] = jnp.dot(hb[i], wd[...], preferred_element_type=F32)
        dd_s[i] = mf[i, pl.ds(pl.multiple_of((1 - core) * 64, 64), 64), :]
        rsend(i, DD, dd_s.at[i], dd_r.at[i], cdev)

    mc = {}

    def I(i):
        rc[i, DD].wait_recv()
        s = mf[i, pl.ds(pl.multiple_of(core * 64, 64), 64), :] + dd_r[i]
        mf[i, :64, :] = s
        mb[i] = s.astype(BF)
        own[zb[i]] = mf[i, :64, pl.ds(pl.multiple_of(chip * 128, 128), 128)]
        for k in range(1, 8):
            g = (chip + k) % 8
            cols = pl.ds(pl.multiple_of(g * 128, 128), 128)
            mc[i, k] = send(mb.at[i, :, cols], mr.at[zb[i], chip], ms.at[i, k], mrs.at[zb[i], chip], chips[k - 1])

    ops = dict(M=M, A=A, B=B, C=C, D=D, E=E, F=F, G=G, I=I)
    for step in " ".join(PLAN).split():
        ops[step[0]](int(step[1:]))

    for b in range(4):
        total = own[b]
        for k in range(1, 8):
            g = (chip + k) % 8
            pltpu.make_async_remote_copy(src_ref=mr.at[b, g], dst_ref=mr.at[b, g], send_sem=ms.at[b, k], recv_sem=mrs.at[b, g],
                                         device_id=chips[k - 1], device_id_type=MESH).wait_recv()
            total = total + mr[b, g].astype(F32)
        fin_s[b] = total.astype(BF)
    fc = send(fin_s, fin_r, fs_sem, fr_sem, cdev)

    def place(v, which):
        for b in range(4):
            vb = v[b]
            sel = jnp.where(core == 0, vb[:, :64].astype(F32), vb[:, 64:].astype(F32)).astype(BF)
            out[pl.ds(pl.multiple_of(b * 128 + which * 64, 64), 64), :] = sel

    place(fin_s, core)
    fc.wait_recv()
    place(fin_r, 1 - core)
    for c in sent:
        c.wait_send()


def body(tokens, gate_weight, up_weight, down_weight):
    d, ff = gate_weight.shape
    vm = pltpu.VMEM
    sem = lambda *s: pltpu.SemaphoreType.DMA(s) if s else pltpu.SemaphoreType.DMA
    piece = lambda: vm((4, 2, 2, 16, ff), BF)
    scratch = [
        vm((d, ff), BF), vm((d, ff), BF), vm((ff, d), BF), vm((8, 4, 1024), BF), vm((4, 128, 1024), BF),
        vm((4, 2, 128, ff), F32), vm((2, 2, 16, ff), F32), piece(), piece(), piece(), piece(), piece(), piece(),
        vm((4, 2, 16, ff), BF), vm((4, 2, 16, ff), BF), vm((4, 2, 16, ff), F32), vm((4, 128, ff), BF),
        vm((4, 128, 1024), F32), vm((4, 64, 1024), F32), vm((4, 64, 1024), F32), vm((4, 64, 1024), BF),
        vm((4, 8, 64, 128), BF), vm((4, 64, 128), F32), vm((4, 64, 128), BF), vm((4, 64, 128), BF),
        sem(3), sem(7), sem(7), sem(3), sem(3), sem(4), sem(4), sem(4, 16), sem(4, 16), sem(4, 8), sem(4, 8),
        sem(), sem(),
    ]
    return pl.pallas_call(
        kernel,
        out_shape=jax.ShapeDtypeStruct((512, 64), BF),
        in_specs=[pl.BlockSpec(memory_space=vm)] + [pl.BlockSpec(memory_space=pl.ANY)] * 3,
        out_specs=pl.BlockSpec(memory_space=vm),
        scratch_shapes=scratch,
        compiler_params=pltpu.CompilerParams(collective_id=0, has_side_effects=True, vmem_limit_bytes=60 * 2**20),
        name="ffn",
    )(tokens, gate_weight, up_weight, down_weight)


def solution(mesh):
    in_specs = (P(("tp", "fs"), None), P("fs", "tp"), P("fs", "tp"), P("tp", "fs"))
    out_specs = P(None, ("fs", "tp"))
    return jax.shard_map(body, mesh=mesh, in_specs=in_specs, out_specs=out_specs, check_vma=False)
```

time: 245 us -> 102 us (0.42)
  blocking collectives: 185 us -> 0 us
  Pallas kernels: 0 us -> 87.4 us
  matrix products: 15.4 us -> 0 us
  waiting for transfers between devices: 15.2 us -> 0 us
  starting transfers between devices: 11 us -> 0 us
    unnamed x2 -> x0, blocking collectives: 110 us -> none
    pallas_call x0 -> x1, Pallas kernels: none -> 87.4 us  [body(): pl.pallas_call(kernel, out_shape=jax.ShapeDtypeStruct((512, 64), BF), in_...]
    all_to_all x3 -> x0, blocking collectives: 75.5 us -> none  [the longest x1 38.2 us: sent_and_summed(): lax.all_to_all(pieces, axis, split_axis=0, concat_axis=0, tiled=True)]
    dot_general x3 -> x0, matrix products: 15.4 us -> none  [the longest x1 6.28 us: body(): jnp.dot(feature_rows, gate_weight, preferred_element_type=jnp.float32)]
    all_to_all x1 -> x0, waiting for transfers between devices: 15.2 us -> none  [copy_for_each(): return lax.all_to_all(copies, axis, split_axis=0, concat_axis=0, tiled=True)]
    unnamed x4 -> x0, starting transfers between devices: 7.45 us -> none
    all_to_all x1 -> x0, starting transfers between devices: 3.59 us -> none  [copy_for_each(): return lax.all_to_all(copies, axis, split_axis=0, concat_axis=0, tiled=True)]
    unnamed x21 -> x2, local copies, waits for them, and re-layouts: 11.8 us -> 12.4 us
  transfers between devices with their start and end apart: 5 -> 0, of which waited for: 1 -> 0; matrix products, arithmetic and copies ran while one was open for 4% -> 0% of each run, Pallas kernels for 0% -> 0%
where the time goes in v1:
time: 102 us; the launch traced here: 101 us
  Pallas kernels  87.4 us (86%)
  local copies, waits for them, and re-layouts  14 us (14%)
    pallas_call x1, Pallas kernels, body(): pl.pallas_call(kernel, out_shape=jax.ShapeDtypeStruct((512, 64), BF), in_...  87.4 us
    unnamed x2, local copies, waits for them, and re-layouts  12.4 us

profile of v1, /device:TPU:1, one launch (start us, length us, event | category | flops | bytes accessed | tf_op | source)
XLA Modules:
  0.0 101.5 jit_solution(11326165796062656890)
XLA Ops:
  0.0 6.2 %copy.5.wg_hbm = bf16[1024,1848]{1,0:T(8,128)(2,1)} copy(bf16[1024,1848]{0,1:T(8,128)(2,1)} %param.5) | data formatting | bytes 7569408 | tf_op args[1]
  6.2 6.2 %copy.6.wu_hbm = bf16[1024,1848]{1,0:T(8,128)(2,1)} copy(bf16[1024,1848]{0,1:T(8,128)(2,1)} %param.6) | data formatting | bytes 7569408 | tf_op args[2]
  12.4 87.4 %ffn.1 = bf16[512,64]{1,0:T(8,128)(2,1)} custom-call(bf16[4,8192]{1,0:T(4,128)(2,1)} %tok.1, bf16[1024,1848]{1,0:T(8,128)(2,1)} %copy.5.wg_hbm, bf16[1024,1848]{1,0:T(8,128)(2,1)} %copy.6.wu_hbm, bf16[1848,1024]{1,0:T(8,128)(2,1)} %wd_hbm.1), custom_call_target="tpu_custom_call" | custom-call | tf_op jit(solution)/shard_map/ffn/pallas_call | solution.py:232
  99.8 1.6 %copy.7 = bf16[512,64]{0,1:T(8,128)(2,1)} copy(bf16[512,64]{1,0:T(8,128)(2,1)} %ffn.1) | data formatting | bytes 131072 | tf_op jit(solution)/shard_map/ffn/pallas_call | solution.py:232

commit v2 on v0

v2 whole, which is shorter than its diff:
```python
import functools

import jax
import jax.numpy as jnp
from jax import lax
from jax.experimental import pallas as pl
from jax.experimental.pallas import tpu as pltpu
from jax.sharding import PartitionSpec as P

BF = jnp.bfloat16
F32 = jnp.float32
MESH = pl.DeviceIdType.MESH

(UF, UE, UL, UX, GX, GF, GE, GL, AX, AY, AP, AQ, AF, AR, DD) = (0, 2, 4, 6, 7, 11, 13, 15, 17, 18, 20, 22, 24, 26, 30)
GL_COLS = 896
P_COLS = 1280
Q_COLS = 1536
PLAN = (
    "t0 g0 u0 r1",
    "r0 b0 g2 c0",
    "u1 f0 u2 g3",
    "d0 c2 w0 b1",
    "e0 g1 b2 u3",
    "e2 d2 b3 h0",
    "c3 c1 d1 e3",
    "h2 e1 d3 i0",
    "i2 h3 j0 h1",
    "j2 i3 i1 k2",
    "j3 k0 j1 l2",
    "l0 k3 k1 l3",
    "l1",
)


def dot_nt(a, b):
    return lax.dot_general(a, b, (((1,), (1,)), ((), ())), preferred_element_type=F32)


def kernel(tok, wg_hbm, wu_hbm, wd_hbm, out, wg_raw, wu_raw, wd_raw, wg, wu, wd, slab, x, pf, uf_s, uf_r, ue_s, ue_r, ul_s, ul_r,
           ux_s, ux_r, gx_s, gx_r, gf_s, gf_r, ge_s, ge_r, gl_s, gl_r, uk, hb, mf, dd_s, dd_r, mb, mr, own,
           wsem, t1s, t1r, zs, zr, rs, rr, ms, mrs):
    f = lax.axis_index("fs")
    t = lax.axis_index("tp")
    y, xl = f // 2, f % 2
    z, xh, core = t // 4, (t // 2) % 2, t % 2
    chip = t // 2
    ff = pf.shape[-1]

    def fs_dev(yy, xx):
        return {"fs": (yy % 4) * 2 + xx, "tp": t}

    def tp_dev(zz, hh, cc):
        return {"fs": f, "tp": (zz % 4) * 4 + hh * 2 + cc}

    loads = [pltpu.make_async_copy(a, b, wsem.at[i]) for i, (a, b) in enumerate(((wu_hbm, wu_raw), (wg_hbm, wg_raw), (wd_hbm, wd_raw)))]
    for c in loads:
        c.start()

    ydev = (fs_dev(y + 1, xl), fs_dev(y + 3, xl))
    xdev = fs_dev(y, 1 - xl)
    cdev = tp_dev(z, xh, 1 - core)
    zdev = (tp_dev(z + 1, xh, core), tp_dev(z + 3, xh, core))
    chips = [{"fs": f, "tp": ((chip + k) % 8) * 2 + core} for k in range(1, 8)]
    quarter = xh * 2 + core
    slot = quarter * 8 + f
    col = xh * 2 + xl
    hops = lambda n: min(n, 4 - n)
    near_last = sorted(((dy, dx, dc) for dy in range(4) for dx in range(4) for dc in range(2)), key=lambda o: -(hops(o[0]) + hops(o[1])))
    plane, owner = [], []
    for dy, dx, dc in near_last[:-2] + [(0, 0, 1)]:
        cx = (col + dx) % 4
        plane.append({"fs": ((y + dy) % 4) * 2 + cx % 2, "tp": z * 4 + (cx // 2) * 2 + (core + dc) % 2})
        owner.append(((y + dy) % 4) * 2 + cx % 2)

    barrier = pltpu.get_barrier_semaphore()
    peers = plane + list(zdev)
    for d in peers:
        pl.semaphore_signal(barrier, inc=1, device_id=d, device_id_type=MESH)
    pl.semaphore_wait(barrier, len(peers))

    sent = []

    def send(src, dst, ssem, rsem, dev):
        c = pltpu.make_async_remote_copy(src_ref=src, dst_ref=dst, send_sem=ssem, recv_sem=rsem, device_id=dev, device_id_type=MESH)
        c.start()
        sent.append(c)
        return c

    t1 = []
    for k in range(31):
        cols = pl.ds(pl.multiple_of(owner[k] * 1024, 1024), 1024)
        t1.append(send(tok.at[:, cols], slab.at[slot], t1s.at[k], t1r.at[k], plane[k]))
    slab[slot] = tok[:, pl.ds(pl.multiple_of(f * 1024, 1024), 1024)]
    for b in range(4):
        mr[b, chip] = jnp.zeros_like(mr[b, chip])
    loads[0].wait()
    wu[...] = wu_raw[...].T
    loads[1].wait()
    wg[...] = wg_raw[...].T

    zb = (z, (z + 3) % 4, (z + 1) % 4, (z + 2) % 4)
    r32 = lambda yy: pl.ds(pl.multiple_of((yy % 4) * 32, 32), 32)
    r16 = lambda yy, xx: pl.ds(pl.multiple_of((yy % 4) * 32 + xx * 16, 16), 16)
    zc = {}

    def zsend(k, block, start, rows, dev):
        part = x.at[block, pl.ds(pl.multiple_of(start, 32), rows)]
        zc[k] = send(part, part, zs.at[k], zr.at[k], dev)

    def first(_):
        for c in t1:
            c.wait_recv()
        x[z] = slab[...].astype(F32).reshape(128, 1024).astype(BF)
        for d in (0, 1):
            zsend(d, z, core * 64, 64, zdev[d])

    def relay(d):
        zc[d].wait_recv()
        zsend(2 + d, zb[1 + d], core * 64, 64, cdev)
        zsend(4 + d, zb[1 + d], core * 64 + 32 * d, 32, zdev[d])

    def relay_far(_):
        for d in (0, 1):
            zc[4 + d].wait_recv()
        zsend(6, zb[3], core * 64, 64, cdev)

    held = {0}

    def tokens(i):
        if i not in held:
            held.add(i)
            zc[(2, 3, 6)[i - 1]].wait_recv()

    def turn(_):
        loads[2].wait()
        wd[...] = wd_raw[...].T

    rc = {}

    def rsend(i, k, src, dst, dev):
        rc[i, k] = send(src, dst, rs.at[i, k], rr.at[i, k], dev)

    def near(d):
        return y + 1 + 2 * d

    lcol, rcol = pl.ds(0, GL_COLS), pl.ds(GL_COLS, ff - GL_COLS)
    gcol = (lcol, rcol)

    def up(i):
        tokens(i)
        pf[i, 1] = jnp.dot(x[zb[i]], wu[...], preferred_element_type=F32)
        for d in (0, 1):
            uf_s[i, d] = pf[i, 1, r16(y + 2, d), :].astype(BF)
            rsend(i, UF + d, uf_s.at[i, d], uf_r.at[i, d], ydev[d])
        for d in (0, 1):
            ue_s[i, d] = pf[i, 1, r16(near(d), 1 - d), :].astype(BF)
            rsend(i, UE + d, ue_s.at[i, d], ue_r.at[i, d], ydev[d])

    def gate(i):
        tokens(i)
        pf[i, 0] = jnp.dot(x[zb[i]], wg[...], preferred_element_type=F32)
        for k, j in enumerate((2, 1, 3, 0)):
            gx_s[i, k] = pf[i, 0, r16(y + j, 1 - xl), :].astype(BF)
            rsend(i, GX + k, gx_s.at[i, k], gx_r.at[i, k], xdev)

    def up_late(i):
        for d in (0, 1):
            rc[i, UF + d].wait_recv()
            ul_s[i, d] = (pf[i, 1, r16(near(d), d), :] + uf_r[i, d].astype(F32)).astype(BF)
            rsend(i, UL + d, ul_s.at[i, d], ul_r.at[i, d], ydev[d])

    def gate_far(i):
        rc[i, GX].wait_recv()
        gf_s[i] = (pf[i, 0, r16(y + 2, xl), :] + gx_r[i, 0].astype(F32)).astype(BF)
        for d in (0, 1):
            rsend(i, GF + d, gf_s.at[i, :, gcol[d]], gf_r.at[i, :, gcol[d]], ydev[d])
        for d in (0, 1):
            rc[i, GX + 1 + d].wait_recv()
            c = gcol[1 - d]
            ge_s[i, d, :, c] = (pf[i, 0, r16(near(d), xl), c] + gx_r[i, 1 + d, :, c].astype(F32)).astype(BF)
            rsend(i, GE + d, ge_s.at[i, d, :, c], ge_r.at[i, d, :, c], ydev[d])

    def up_pair(i):
        for k in (UE, UE + 1, UL, UL + 1):
            rc[i, k].wait_recv()
        s0 = pf[i, 1, r16(y, 0), :] + ul_r[i, 0].astype(F32) + ue_r[i, 1].astype(F32)
        s1 = pf[i, 1, r16(y, 1), :] + ue_r[i, 0].astype(F32) + ul_r[i, 1].astype(F32)
        ux_s[i] = jnp.where(xl == 0, s1, s0).astype(BF)
        rsend(i, UX, ux_s.at[i], ux_r.at[i], xdev)
        uk[i] = jnp.where(xl == 0, s0, s1)

    def gate_late(i):
        for d in (0, 1):
            rc[i, GF + d].wait_recv()
            c = gcol[d]
            gl_s[i, d, :, c] = (pf[i, 0, r16(near(d), xl), c] + gx_r[i, 1 + d, :, c].astype(F32) + gf_r[i, :, c].astype(F32)).astype(BF)
            rsend(i, GL + d, gl_s.at[i, d, :, c], gl_r.at[i, d, :, c], ydev[d])

    pcol, qcol = pl.ds(0, P_COLS), pl.ds(P_COLS, ff - P_COLS)
    qhalf = (pl.ds(P_COLS, Q_COLS - P_COLS), pl.ds(Q_COLS, ff - Q_COLS))

    def hid(i):
        for k in (GX + 3, GE, GE + 1, GL, GL + 1, UX):
            rc[i, k].wait_recv()
        u = uk[i] + ux_r[i].astype(F32)
        for d in (0, 1):
            c = gcol[d]
            g = pf[i, 0, r16(y, xl), c] + gx_r[i, 3, :, c].astype(F32) + gl_r[i, d, :, c].astype(F32) + ge_r[i, 1 - d, :, c].astype(F32)
            uc = u[:, :GL_COLS] if d == 0 else u[:, GL_COLS:]
            hb[i, r16(y, xl), c] = (g / (1.0 + jnp.exp(-g)) * uc).astype(BF)
        mine = r16(y, xl)
        p, q = hb.at[i, mine, pcol], hb.at[i, mine, qcol]
        rsend(i, AX, p, p, xdev)
        for d in (0, 1):
            rsend(i, AY + d, q, q, ydev[d])
        rsend(i, AR, q, q, xdev)

    def spread(i):
        rc[i, AX].wait_recv()
        pair = hb.at[i, r32(y), pcol]
        for d in (0, 1):
            rsend(i, AP + d, pair, pair, ydev[d])
        for d in (0, 1):
            rc[i, AY + d].wait_recv()
            row = r16(near(1 - d), xl)
            part, whole = hb.at[i, row, qhalf[d]], hb.at[i, row, qcol]
            rsend(i, AQ + d, part, part, ydev[d])
            rsend(i, AR + 1 + d, whole, whole, xdev)

    def spread_far(i):
        for d in (0, 1):
            rc[i, AP + d].wait_recv()
            part = hb.at[i, r16(near(1 - d), d), pcol]
            rsend(i, AF + d, part, part, ydev[d])
        for d in (0, 1):
            rc[i, AQ + d].wait_recv()
        whole = hb.at[i, r16(y + 2, xl), qcol]
        rsend(i, AR + 3, whole, whole, xdev)

    def arrived(i):
        for k in (AF, AF + 1, AR, AR + 1, AR + 2, AR + 3):
            rc[i, k].wait_recv()

    def halves(i):
        dd_s[i] = mf[i, :, 1 - core]
        rsend(i, DD, dd_s.at[i], dd_r.at[i], cdev)

    def down(i):
        arrived(i)
        mf[i] = dot_nt(wd[...], hb[i]).reshape(8, 2, 64, 128)
        halves(i)

    def down_two(i):
        arrived(i)
        arrived(i + 1)
        both = dot_nt(wd[...], hb[i : i + 2].reshape(256, ff))
        for j in (0, 1):
            mf[i + j] = both[:, j * 128 : (j + 1) * 128].reshape(8, 2, 64, 128)
            halves(i + j)

    mc = {}

    def columns(i):
        rc[i, DD].wait_recv()
        mf[i, :, core] = mf[i, :, core] + dd_r[i]
        mb[i] = mf[i, :, core].astype(BF)
        own[zb[i]] = mf[i, chip, core]
        for k in range(1, 8):
            g = (chip + k) % 8
            mc[i, k] = send(mb.at[i, g], mr.at[zb[i], chip], ms.at[i, k], mrs.at[zb[i], chip], chips[k - 1])

    def collect(b, m):
        g = (b * 2 + 4 + m) % 8

        @pl.when(g != chip)
        def _():
            pltpu.make_async_remote_copy(src_ref=mr.at[b, g], dst_ref=mr.at[b, g], send_sem=ms.at[b, 0], recv_sem=mrs.at[b, g],
                                         device_id=chips[0], device_id_type=MESH).wait_recv()

        return mr[b, g].astype(F32)

    ops = dict(t=first, r=relay, f=relay_far, w=turn, u=up, g=gate, b=up_late, c=gate_far, d=up_pair, e=gate_late, h=hid,
               i=spread, j=spread_far, k=down, K=down_two, l=columns)
    for step in " ".join(PLAN).split():
        ops[step[0]](int(step[1:]))

    for b in range(4):
        own[b] = own[b] + sum(collect(b, m) for m in range(2, 8))
    for b in range(4):
        out[:, b * 128 : (b + 1) * 128] = (own[b] + collect(b, 0) + collect(b, 1)).astype(BF)
    for c in sent:
        c.wait_send()


def body(tokens, gate_weight, up_weight, down_weight):
    d, ff = gate_weight.shape
    vm = pltpu.VMEM
    sem = lambda *s: pltpu.SemaphoreType.DMA(s) if s else pltpu.SemaphoreType.DMA
    piece = lambda: vm((4, 2, 16, ff), BF)
    one = lambda: vm((4, 16, ff), BF)
    scratch = [
        vm((ff, d), BF), vm((ff, d), BF), vm((ff, d), BF), vm((d, ff), BF), vm((d, ff), BF), vm((d, ff), BF), vm((32, 4, 1024), BF), vm((4, 128, 1024), BF),
        vm((4, 2, 128, ff), F32), piece(), piece(), piece(), piece(), piece(), piece(), one(), one(),
        vm((4, 4, 16, ff), BF), vm((4, 4, 16, ff), BF), one(), one(), piece(), piece(), piece(), piece(),
        vm((4, 16, ff), F32), vm((4, 128, ff), BF),
        vm((4, 8, 2, 64, 128), F32), vm((4, 8, 64, 128), F32), vm((4, 8, 64, 128), F32), vm((4, 8, 64, 128), BF),
        vm((4, 8, 64, 128), BF), vm((4, 64, 128), F32),
        sem(3), sem(31), sem(31), sem(7), sem(7), sem(4, 31), sem(4, 31), sem(4, 8), sem(4, 8),
    ]
    return pl.pallas_call(
        kernel,
        out_shape=jax.ShapeDtypeStruct((64, 512), BF),
        in_specs=[pl.BlockSpec(memory_space=vm)] + [pl.BlockSpec(memory_space=pl.ANY)] * 3,
        out_specs=pl.BlockSpec(memory_space=vm),
        scratch_shapes=scratch,
        compiler_params=pltpu.CompilerParams(collective_id=0, has_side_effects=True, vmem_limit_bytes=60 * 2**20),
        name="ffn",
    )(tokens, gate_weight.T, up_weight.T, down_weight).T


def solution(mesh):
    in_specs = (P(("tp", "fs"), None), P("fs", "tp"), P("fs", "tp"), P("tp", "fs"))
    out_specs = P(None, ("fs", "tp"))
    return jax.shard_map(body, mesh=mesh, in_specs=in_specs, out_specs=out_specs, check_vma=False)
```

time: 245 us -> 77.3 us (0.32)
  blocking collectives: 185 us -> 0 us
  Pallas kernels: 0 us -> 75.6 us
  matrix products: 15.4 us -> 0 us
  waiting for transfers between devices: 15.2 us -> 0 us
  local copies, waits for them, and re-layouts: 15.2 us -> 1.47 us
  starting transfers between devices: 11 us -> 0 us
    unnamed x2 -> x0, blocking collectives: 110 us -> none
    pallas_call x0 -> x1, Pallas kernels: none -> 75.6 us  [body(): pl.pallas_call(kernel, out_shape=jax.ShapeDtypeStruct((64, 512), BF), in_...]
    all_to_all x3 -> x0, blocking collectives: 75.5 us -> none  [the longest x1 38.2 us: sent_and_summed(): lax.all_to_all(pieces, axis, split_axis=0, concat_axis=0, tiled=True)]
    dot_general x3 -> x0, matrix products: 15.4 us -> none  [the longest x1 6.28 us: body(): jnp.dot(feature_rows, gate_weight, preferred_element_type=jnp.float32)]
    all_to_all x1 -> x0, waiting for transfers between devices: 15.2 us -> none  [copy_for_each(): return lax.all_to_all(copies, axis, split_axis=0, concat_axis=0, tiled=True)]
    unnamed x21 -> x1, local copies, waits for them, and re-layouts: 11.8 us -> 1.47 us
    unnamed x4 -> x0, starting transfers between devices: 7.45 us -> none
    all_to_all x1 -> x0, starting transfers between devices: 3.59 us -> none  [copy_for_each(): return lax.all_to_all(copies, axis, split_axis=0, concat_axis=0, tiled=True)]
  transfers between devices with their start and end apart: 5 -> 0, of which waited for: 1 -> 0; matrix products, arithmetic and copies ran while one was open for 4% -> 0% of each run, Pallas kernels for 0% -> 0%
where the time goes in v2:
time: 77.3 us; the launch traced here: 77.1 us
  Pallas kernels  75.6 us (98%)
  local copies, waits for them, and re-layouts  1.47 us (2%)
    pallas_call x1, Pallas kernels, body(): pl.pallas_call(kernel, out_shape=jax.ShapeDtypeStruct((64, 512), BF), in_...  75.6 us

profile of v2, /device:TPU:1, one launch (start us, length us, event | category | flops | bytes accessed | tf_op | source)
XLA Modules:
  0.0 77.1 jit_solution(13032695912059518737)
XLA Ops:
  0.0 75.6 %ffn.1 = bf16[64,512]{1,0:T(8,128)(2,1)} custom-call(bf16[4,8192]{1,0:T(4,128)(2,1)} %tok.1, bf16[1848,1024]{1,0:T(8,128)(2,1)} %bitcast.3, bf16[1848,1024]{1,0:T(8,128)(2,1)} %bitcast.4, bf16[1848,1024]{1,0:T(8,128)(2,1)} %wd_hbm.1), custom_call_target="tpu_custom_call" | custom-call | tf_op jit(solution)/shard_map/ffn/pallas_call | solution.py:310
  75.6 1.5 %copy.6 = bf16[512,64]{0,1:T(8,128)(2,1)} copy(bf16[512,64]{0,1:T(8,128)(2,1)} %bitcast.5) | data formatting | bytes 131072

commit v3 on v2

--- a/solution.py
+++ b/solution.py
@@ -36,7 +36,7 @@
     return lax.dot_general(a, b, (((1,), (1,)), ((), ())), preferred_element_type=F32)
 
 
-def kernel(tok, wg_hbm, wu_hbm, wd_hbm, out, wg_raw, wu_raw, wd_raw, wg, wu, wd, slab, x, pf, uf_s, uf_r, ue_s, ue_r, ul_s, ul_r,
+def kernel(tok_hbm, wg_hbm, wu_hbm, wd_hbm, out, tok, wg_raw, wu_raw, wd_raw, wg, wu, wd, slab, x, pf, uf_s, uf_r, ue_s, ue_r, ul_s, ul_r,
            ux_s, ux_r, gx_s, gx_r, gf_s, gf_r, ge_s, ge_r, gl_s, gl_r, uk, hb, mf, dd_s, dd_r, mb, mr, own,
            wsem, t1s, t1r, zs, zr, rs, rr, ms, mrs):
     f = lax.axis_index("fs")
@@ -52,9 +52,9 @@
     def tp_dev(zz, hh, cc):
         return {"fs": f, "tp": (zz % 4) * 4 + hh * 2 + cc}
 
-    loads = [pltpu.make_async_copy(a, b, wsem.at[i]) for i, (a, b) in enumerate(((wu_hbm, wu_raw), (wg_hbm, wg_raw), (wd_hbm, wd_raw)))]
-    for c in loads:
-        c.start()
+    loads = [pltpu.make_async_copy(a, b, wsem.at[i]) for i, (a, b) in enumerate(((wu_hbm, wu_raw), (wg_hbm, wg_raw), (wd_hbm, wd_raw), (tok_hbm, tok)))]
+    for k in (3, 0, 1, 2):
+        loads[k].start()
 
     ydev = (fs_dev(y + 1, xl), fs_dev(y + 3, xl))
     xdev = fs_dev(y, 1 - xl)
@@ -86,6 +86,7 @@
         sent.append(c)
         return c
 
+    loads[3].wait()
     t1 = []
     for k in range(31):
         cols = pl.ds(pl.multiple_of(owner[k] * 1024, 1024), 1024)
@@ -299,21 +300,21 @@
     piece = lambda: vm((4, 2, 16, ff), BF)
     one = lambda: vm((4, 16, ff), BF)
     scratch = [
-        vm((ff, d), BF), vm((ff, d), BF), vm((ff, d), BF), vm((d, ff), BF), vm((d, ff), BF), vm((d, ff), BF), vm((32, 4, 1024), BF), vm((4, 128, 1024), BF),
+        vm((4, 8192), BF), vm((ff, d), BF), vm((ff, d), BF), vm((ff, d), BF), vm((d, ff), BF), vm((d, ff), BF), vm((d, ff), BF), vm((32, 4, 1024), BF), vm((4, 128, 1024), BF),
         vm((4, 2, 128, ff), F32), piece(), piece(), piece(), piece(), piece(), piece(), one(), one(),
         vm((4, 4, 16, ff), BF), vm((4, 4, 16, ff), BF), one(), one(), piece(), piece(), piece(), piece(),
         vm((4, 16, ff), F32), vm((4, 128, ff), BF),
         vm((4, 8, 2, 64, 128), F32), vm((4, 8, 64, 128), F32), vm((4, 8, 64, 128), F32), vm((4, 8, 64, 128), BF),
         vm((4, 8, 64, 128), BF), vm((4, 64, 128), F32),
-        sem(3), sem(31), sem(31), sem(7), sem(7), sem(4, 31), sem(4, 31), sem(4, 8), sem(4, 8),
+        sem(4), sem(31), sem(31), sem(7), sem(7), sem(4, 31), sem(4, 31), sem(4, 8), sem(4, 8),
     ]
     return pl.pallas_call(
         kernel,
         out_shape=jax.ShapeDtypeStruct((64, 512), BF),
-        in_specs=[pl.BlockSpec(memory_space=vm)] + [pl.BlockSpec(memory_space=pl.ANY)] * 3,
+        in_specs=[pl.BlockSpec(memory_space=pl.ANY)] * 4,
         out_specs=pl.BlockSpec(memory_space=vm),
         scratch_shapes=scratch,
-        compiler_params=pltpu.CompilerParams(collective_id=0, has_side_effects=True, vmem_limit_bytes=60 * 2**20),
+        compiler_params=pltpu.CompilerParams(collective_id=0, has_side_effects=True, vmem_limit_bytes=52 * 2**20),
         name="ffn",
     )(tokens, gate_weight.T, up_weight.T, down_weight).T
 

time: 77.3 us -> 76 us (0.983)
  Pallas kernels: 75.6 us -> 74.3 us
    pallas_call x1, Pallas kernels: 75.6 us -> 74.3 us  [body(): pl.pallas_call(kernel, out_shape=jax.ShapeDtypeStruct((64, 512), BF), in_...]
where the time goes in v3:
time: 76 us; the launch traced here: 75.8 us
  Pallas kernels  74.3 us (98%)
  local copies, waits for them, and re-layouts  1.47 us (2%)
    pallas_call x1, Pallas kernels, body(): pl.pallas_call(kernel, out_shape=jax.ShapeDtypeStruct((64, 512), BF), in_...  74.3 us

profile of v3, /device:TPU:1, one launch (start us, length us, event | category | flops | bytes accessed | tf_op | source)
XLA Modules:
  0.0 75.8 jit_solution(14996268873598219073)
XLA Ops:
  0.0 0.0 copy-start
  0.0 0.8 %copy-done = bf16[4,8192]{1,0:T(4,128)(2,1)S(1)} copy-done((bf16[4,8192]{1,0:T(4,128)(2,1)S(1)}, bf16[4,8192]{1,0:T(4,128)(2,1)}, u32[]{:S(2)}) %copy-start) | copy-done | bytes 65560
  0.8 74.3 %ffn.1 = bf16[64,512]{1,0:T(8,128)(2,1)S(1)} custom-call(bf16[4,8192]{1,0:T(4,128)(2,1)S(1)} %copy-done, bf16[1848,1024]{1,0:T(8,128)(2,1)} %bitcast.4, bf16[1848,1024]{1,0:T(8,128)(2,1)} %bitcast.5, bf16[1848,1024]{1,0:T(8,128)(2,1)} %wd_hbm.1), custom_call_target="tpu_custom_call" | custom-call | tf_op jit(solution)/shard_map/ffn/pallas_call | solution.py:311
  75.2 0.6 copy.6
Async XLA Ops:
  0.0 0.8 %copy-start = (bf16[4,8192]{1,0:T(4,128)(2,1)S(1)}, bf16[4,8192]{1,0:T(4,128)(2,1)}, u32[]{:S(2)}) copy-start(bf16[4,8192]{1,0:T(4,128)(2,1)} %tok_hbm.1) | copy-start | bytes 196612

commit v4 on v3

--- a/solution.py
+++ b/solution.py
@@ -17,18 +17,18 @@
 Q_COLS = 1536
 PLAN = (
     "t0 g0 u0 r1",
-    "r0 b0 g2 c0",
-    "u1 f0 u2 g3",
-    "d0 c2 w0 b1",
-    "e0 g1 b2 u3",
-    "e2 d2 b3 h0",
-    "c3 c1 d1 e3",
-    "h2 e1 d3 i0",
-    "i2 h3 j0 h1",
-    "j2 i3 i1 k2",
-    "j3 k0 j1 l2",
-    "l0 k3 k1 l3",
-    "l1",
+    "g2 b0 c0 r0",
+    "u2 g1 f0 e0",
+    "c2 d0 b2 u1",
+    "g3 u3 d2 b1",
+    "e2 c1 h0 b3",
+    "d1 c3 e1 h2",
+    "i0 e3 d3 h1",
+    "i2 j0 h3 i1",
+    "j2 i3 w0 k0",
+    "j1 k2 j3 l2",
+    "l0 k1 k3 l1",
+    "l3",
 )
 
 

time: 76 us -> 75.3 us (level)
  no operation moved by 1% of the time
where the time goes in v4:
time: 75.3 us; the launch traced here: 75.2 us
  Pallas kernels  73.7 us (98%)
  local copies, waits for them, and re-layouts  1.47 us (2%)
    pallas_call x1, Pallas kernels, body(): pl.pallas_call(kernel, out_shape=jax.ShapeDtypeStruct((64, 512), BF), in_...  73.7 us

profile of v4, /device:TPU:1, one launch (start us, length us, event | category | flops | bytes accessed | tf_op | source)
XLA Modules:
  0.0 75.2 jit_solution(6630096499415521414)
XLA Ops:
  0.0 0.0 copy-start
  0.0 0.8 %copy-done = bf16[4,8192]{1,0:T(4,128)(2,1)S(1)} copy-done((bf16[4,8192]{1,0:T(4,128)(2,1)S(1)}, bf16[4,8192]{1,0:T(4,128)(2,1)}, u32[]{:S(2)}) %copy-start) | copy-done | bytes 65560
  0.8 73.7 %ffn.1 = bf16[64,512]{1,0:T(8,128)(2,1)S(1)} custom-call(bf16[4,8192]{1,0:T(4,128)(2,1)S(1)} %copy-done, bf16[1848,1024]{1,0:T(8,128)(2,1)} %bitcast.4, bf16[1848,1024]{1,0:T(8,128)(2,1)} %bitcast.5, bf16[1848,1024]{1,0:T(8,128)(2,1)} %wd_hbm.1), custom_call_target="tpu_custom_call" | custom-call | tf_op jit(solution)/shard_map/ffn/pallas_call | solution.py:311
  74.6 0.6 copy.6
Async XLA Ops:
  0.0 0.8 %copy-start = (bf16[4,8192]{1,0:T(4,128)(2,1)S(1)}, bf16[4,8192]{1,0:T(4,128)(2,1)}, u32[]{:S(2)}) copy-start(bf16[4,8192]{1,0:T(4,128)(2,1)} %tok_hbm.1) | copy-start | bytes 196612
